TPU v7x, 32 devices: a whole 2x2x4 slice. The times are simulated.
32 devices in a mesh: seq: 8 (over z, y), samp: 4 (over x, core).
Axes of the slice: x: 2, y: 2, z: 4, core: 2. Of those that a mesh axis runs over, the one named last changes fastest.
Arguments:
- queries: bfloat16 [4, 1024, 5120], P('samp', 'seq'), may hold values from -120 to 120
- prefix_keys: bfloat16 [1024, 1024], P('seq'), may hold values from -4 to 4
- prefix_values: bfloat16 [1024, 1024], P('seq'), may hold values from -4 to 4
- suffix_keys: bfloat16 [4, 1024, 1024], P('samp', 'seq'), may hold values from -5 to 5
- suffix_values: bfloat16 [4, 1024, 1024], P('samp', 'seq'), may hold values from -4 to 4
- layout_pre: int32 [4, 8, 8], P('samp', 'seq'), may hold values 0 or 1
- layout_suf: int32 [4, 8, 8], P('samp', 'seq'), may hold values 0 or 1
- lengths: int32 [4], P('samp'), may hold values from 1 to 8
Outputs:
- attended: bfloat16 [4, 1024, 5120], P('samp', 'seq')
All inputs are finite; a program needn't handle non-finite values. No bound on the sum of `layout_pre` or of `layout_suf` on one device may be relied on, other than what follows from the above.
Results may differ from a plain program's by a relative error of at most 0.004.
Values may be sent and summed in bfloat16 or wider, within the bound.
No kernel may reach another device: no remote copies, remote signals or barrier semaphores. Data moves between devices by JAX's collectives and lax.ppermute only.
A program may use at most 128 MiB of HBM per device.

v0:
```python
import math
import jax
import jax.numpy as jnp
from jax import lax
from jax.sharding import PartitionSpec as P

HEADS = 40
KV_HEADS = 8
HEAD_DIM = 128
BLOCK = 128
masked_value = -1e30


def block_size(count):
    return math.gcd(count, 512)


def softmax_step(carry, scores, allowed, value_rows, form):
    run_max, run_sum, run_total = carry
    key_mask = allowed[:, None, None, :, :]
    block_max = jnp.max(jnp.where(key_mask, scores, masked_value), axis=-1)
    new_max = jnp.maximum(run_max, block_max)
    weights = jnp.where(key_mask, jnp.exp(scores - new_max[..., None]), 0.0)
    scale_old = jnp.exp(run_max - new_max)
    new_sum = run_sum * scale_old + jnp.sum(weights, axis=-1)
    rounded = weights.astype(jnp.bfloat16)
    added = jnp.einsum(form, rounded, value_rows, preferred_element_type=jnp.float32)
    rescale = jnp.transpose(scale_old, (0, 3, 1, 2))[..., None]
    return (new_max, new_sum, run_total * rescale + added)


def lookup(table, block_ids):
    columns = jnp.arange(table.shape[1], dtype=jnp.int32)
    onehot = (block_ids[None, :] == columns[:, None]).astype(jnp.int32)
    return jnp.sum(table[:, :, None] * onehot[None, :, :], axis=1) > 0


def shards(
    queries, prefix_keys, prefix_values, suffix_keys, suffix_values, layout_pre, layout_suf, lengths
):
    group_size = HEADS // KV_HEADS
    score_scale = 1.0 / math.sqrt(HEAD_DIM)
    samples = queries.shape[0]
    query_block = lax.axis_index("seq")
    query_grid = queries.reshape(samples, BLOCK, KV_HEADS, group_size, HEAD_DIM)
    query_position = query_block * BLOCK + jnp.arange(BLOCK, dtype=jnp.int32)
    pre_table = layout_pre[:, 0, :]
    suf_table = layout_suf[:, 0, :]
    start_carry = (
        jnp.full((samples, KV_HEADS, group_size, BLOCK), masked_value, jnp.float32),
        jnp.zeros((samples, KV_HEADS, group_size, BLOCK), jnp.float32),
        jnp.zeros((samples, BLOCK, KV_HEADS, group_size, HEAD_DIM), jnp.float32),
    )
    share = prefix_keys.shape[0] // lax.axis_size("samp")
    seq_count = lax.axis_size("seq")
    shard_rows = prefix_keys.shape[0]
    share_start = lax.axis_index("samp") * share
    own_keys = lax.dynamic_slice_in_dim(prefix_keys, share_start, share, 0)
    own_values = lax.dynamic_slice_in_dim(prefix_values, share_start, share, 0)
    shares = (
        lax.all_gather(own_keys, "seq", axis=0, tiled=True),
        lax.all_gather(own_values, "seq", axis=0, tiled=True),
    )
    pieces = (
        lax.all_gather(shares[0], "samp", axis=0, tiled=True),
        lax.all_gather(shares[1], "samp", axis=0, tiled=True),
    )
    whole_index = jnp.arange(pieces[0].shape[0], dtype=jnp.int32)
    owner_share = whole_index // (seq_count * share)
    remainder = whole_index % (seq_count * share)
    positions = remainder // share * shard_rows + owner_share * share + remainder % share
    carry = start_carry
    key_rows = pieces[0]
    value_rows = pieces[1]
    count = key_rows.shape[0]
    prefix_size = block_size(count)
    steps = count // prefix_size

    def prefix_one_step(inner, pieces):
        key_part, value_part, place = pieces
        key_grid = key_part.reshape(prefix_size, KV_HEADS, HEAD_DIM)
        value_grid = value_part.reshape(prefix_size, KV_HEADS, HEAD_DIM)
        scores = (
            jnp.einsum("sqgjd,rgd->sgjqr", query_grid, key_grid, preferred_element_type=jnp.float32)
            * score_scale
        )
        seen = lookup(pre_table, place // BLOCK)
        allowed = jnp.broadcast_to(seen[:, None, :], (samples, BLOCK, prefix_size))
        return (softmax_step(inner, scores, allowed, value_grid, "sgjqr,rgd->sqgjd"), None)

    width = key_rows.shape[1]
    carry, unused = lax.scan(
        prefix_one_step,
        carry,
        (
            key_rows.reshape(steps, prefix_size, width),
            value_rows.reshape(steps, prefix_size, width),
            positions.reshape(steps, prefix_size),
        ),
    )
    suffix_carry = carry
    key_rows = lax.all_gather(suffix_keys, "seq", axis=1, tiled=True)
    value_rows = lax.all_gather(suffix_values, "seq", axis=1, tiled=True)
    count = key_rows.shape[1]
    size = block_size(count)
    steps = count // size
    width = key_rows.shape[2]
    positions = jnp.arange(count, dtype=jnp.int32).reshape(steps, size)

    def suffix_one_step(inner, items):
        key_part, value_part, place = items
        key_grid = key_part.reshape(samples, size, KV_HEADS, HEAD_DIM)
        value_grid = value_part.reshape(samples, size, KV_HEADS, HEAD_DIM)
        scores = (
            jnp.einsum(
                "sqgjd,srgd->sgjqr", query_grid, key_grid, preferred_element_type=jnp.float32
            )
            * score_scale
        )
        key_block = place // BLOCK
        block_seen = (key_block == query_block)[None, :] | lookup(suf_table, key_block)
        causal = place[None, :] <= query_position[:, None]
        allowed = block_seen[:, None, :] & causal[None, :, :]
        return (softmax_step(inner, scores, allowed, value_grid, "sgjqr,srgd->sqgjd"), None)

    key_steps = jnp.transpose(key_rows.reshape(samples, steps, size, width), (1, 0, 2, 3))
    value_steps = jnp.transpose(value_rows.reshape(samples, steps, size, width), (1, 0, 2, 3))
    suffix_carry, unused = lax.scan(
        suffix_one_step, suffix_carry, (key_steps, value_steps, positions)
    )
    carry = suffix_carry
    run_max, run_sum, run_total = carry
    mixed = run_total / jnp.transpose(run_sum, (0, 3, 1, 2))[..., None]
    mixed = mixed.reshape(samples, BLOCK, HEADS * HEAD_DIM)
    is_live = (query_block < lengths)[:, None, None]
    return jnp.where(is_live, mixed, 0.0).astype(jnp.bfloat16)


def solution(mesh):
    return jax.shard_map(
        shards,
        mesh=mesh,
        in_specs=(
            P("samp", "seq", None),
            P("seq", None),
            P("seq", None),
            P("samp", "seq", None),
            P("samp", "seq", None),
            P("samp", "seq", None),
            P("samp", "seq", None),
            P("samp"),
        ),
        out_specs=P("samp", "seq", None),
        check_vma=False,
    )
```

profile of v0, /device:TPU:0, one launch (start us, length us, event | category | flops | bytes accessed | tf_op | source)
XLA Modules:
  0.0 262.5 jit_solution(15586592918994311306)
XLA Ops:
  6.5 0.0 copy-start
  6.5 0.9 copy-done
  7.5 35.3 %all_gather.18 = bf16[256,1024]{1,0:T(8,128)(2,1)} all-gather(bf16[32,1024]{1,0:T(8,128)(2,1)S(1)} %constant_dynamic-slice_fusion.6), channel_id=1, replica_groups=mesh['seq'=8,'samp'=4] {'seq'}, dimensions={0}, use_global_device_ids=true | all-gather | bytes 589824 | tf_op jit(solution)/shard_map/all_gather | solution.py:61
  42.7 0.0 all-gather.5.cloned.1.call-update
  42.8 0.0 all-gather.7.cloned.1.call-start
  42.8 0.9 constant_dynamic-slice_fusion.5
  43.7 33.2 %all_gather.20 = bf16[256,1024]{1,0:T(8,128)(2,1)} all-gather(bf16[32,1024]{1,0:T(8,128)(2,1)S(1)} %constant_dynamic-slice_fusion.5), channel_id=1, replica_groups=mesh['seq'=8,'samp'=4] {'seq'}, dimensions={0}, use_global_device_ids=true | all-gather | bytes 589824 | tf_op jit(solution)/shard_map/all_gather | solution.py:62
  76.9 0.0 all-gather.7.cloned.1.call-update
  76.9 0.0 all-gather.9.cloned.1.call-start
  76.9 0.7 all-gather.9.cloned.1.call-update
  77.6 0.0 all-gather.11.cloned.1.call-start
  77.7 0.5 all-gather.11.cloned.1.call-update
  78.3 0.0 copy-start.2
  78.3 0.8 copy.38
  79.1 1.4 copy.40
  81.2 0.0 all-gather.5.cloned.1.call-done
  81.2 19.7 %all-gather.7.cloned.1.call-done = bf16[1024,1024]{1,0:T(8,128)(2,1)} async-done(((bf16[256,1024]{1,0:T(8,128)(2,1)}), bf16[1024,1024]{1,0:T(8,128)(2,1)}) %all-gather.7.cloned.1.call-update) | async-done | bytes 2097168 | tf_op jit(solution)/shard_map/all_gather | solution.py:66
  100.9 45.4 %while.35 = (s32[]{:T(128)}, f32[1,8,5,128]{3,2,1,0:T(8,128)S(1)}, f32[1,8,5,128]{3,2,1,0:T(8,128)}, f32[1,128,8,5,128]{1,4,3,2,0:T(8,128)}, s32[2,512]{1,0:T(2,...) while((s32[]{:T(128)}, f32[1,8,5,128]{3,2,1,0:T(8,128)S(1)}, ...), condition=%wide.region_4.5_spmd.clone, body=%wide.region_0.4_spmd.clone.sunk | while | flops 1373029888 | bytes 80294112 | solution.py:92
  100.9 0.1 select_reduce_fusion.5
  101.0 1.7 constant_dynamic-slice_fusion.11
  102.7 0.5 copy.66
  103.3 6.7 %fusion.66 = (f32[8,5,128]{2,1,0:T(8,128)S(1)}, f32[8,512,128,5]{2,1,3,0:T(8,128)}) fusion(pred[512]{0:T(512)(128)(4,1)S(1)} %broadcast_compare_fusion.5, bf16[512,8,128,1]{0,2,3,1:T(8,128)(2,1)S(1)} %bitcast.194, bf16[1,128,8,5,128]{4,1,3,2,0:T(8,128)(2,1)} %get-tuple-element.613), kind=kOutput, calls=%fused_computation.3.clone.1 | convolution fusion | flops 678947840 | bytes 12866048 | tf_op jit(solution)/shard_map/while/body/eval_jaxpr/sqgjd,rgd->sgjqr/dot_general | solution.py:84
  110.0 0.0 slice-start.3
  110.0 1.4 copy.67
  111.4 8.5 %bitcast_add_fusion.11 = f32[1,128,8,5,128]{1,4,3,2,0:T(8,128)} fusion(f32[1,128,8,5,128]{1,4,3,2,0:T(8,128)} %get-tuple-element.598, bf16[512,8,128,1]{0,2,3,1:T(8,128)(2,1)} %bitcast.197, f32[8,512,128,5]{2,1,3,0:T(8,128)} %get-tuple-element.581, f32[8,5,128]{2,1,0:T(8,128)S(1)} %bitcast.200, pred[512]{0:T(512)(128)(4,1)S(1)} %broadcast_compare_fusion.5, ...), kind=kOutput, calls=%fused_computation.14.clone.1 | convolution fusion | flops 683540480 | bytes 16818688 | tf_op jit(solution)/shard_map/while/body/eval_jaxpr/sgjqr,rgd->sqgjd/dot_general | solution.py:27
  119.8 0.0 slice-done.3
  119.8 2.3 fusion.68
  122.1 0.6 bitcast_add_fusion.10
  122.8 0.1 select_reduce_fusion.5
  122.9 1.7 constant_dynamic-slice_fusion.11
  124.6 0.5 copy.66
  125.2 6.8 %fusion.66 = (f32[8,5,128]{2,1,0:T(8,128)S(1)}, f32[8,512,128,5]{2,1,3,0:T(8,128)}) fusion(pred[512]{0:T(512)(128)(4,1)S(1)} %broadcast_compare_fusion.5, bf16[512,8,128,1]{0,2,3,1:T(8,128)(2,1)S(1)} %bitcast.194, bf16[1,128,8,5,128]{4,1,3,2,0:T(8,128)(2,1)} %get-tuple-element.613), kind=kOutput, calls=%fused_computation.3.clone.1 | convolution fusion | flops 678947840 | bytes 12866048 | tf_op jit(solution)/shard_map/while/body/eval_jaxpr/sqgjd,rgd->sgjqr/dot_general | solution.py:84
  132.0 0.0 slice-start.3
  132.0 1.4 copy.67
  133.3 9.2 %bitcast_add_fusion.11 = f32[1,128,8,5,128]{1,4,3,2,0:T(8,128)} fusion(f32[1,128,8,5,128]{1,4,3,2,0:T(8,128)} %get-tuple-element.598, bf16[512,8,128,1]{0,2,3,1:T(8,128)(2,1)} %bitcast.197, f32[8,512,128,5]{2,1,3,0:T(8,128)} %get-tuple-element.581, f32[8,5,128]{2,1,0:T(8,128)S(1)} %bitcast.200, pred[512]{0:T(512)(128)(4,1)S(1)} %broadcast_compare_fusion.5, ...), kind=kOutput, calls=%fused_computation.14.clone.1 | convolution fusion | flops 683540480 | bytes 16818688 | tf_op jit(solution)/shard_map/while/body/eval_jaxpr/sgjqr,rgd->sqgjd/dot_general | solution.py:27
  142.6 2.3 fusion.68
  144.9 1.4 bitcast_add_fusion.10
  146.3 5.9 %all-gather.9.cloned.1.call-done = bf16[1,1024,1024]{2,1,0:T(8,128)(2,1)} async-done(((bf16[1,128,1024]{2,1,0:T(8,128)(2,1)}), bf16[1,1024,1024]{2,1,0:T(8,128)(2,1)}) %all-gather.9.cloned.1.call-update) | async-done | bytes 2097168 | tf_op jit(solution)/shard_map/all_gather | solution.py:102
  152.2 49.6 %all-gather.11.cloned.1.call-done = bf16[1,1024,1024]{2,1,0:T(8,128)(2,1)} async-done(((bf16[1,128,1024]{2,1,0:T(8,128)(2,1)}), bf16[1,1024,1024]{2,1,0:T(8,128)(2,1)}) %all-gather.11.cloned.1.call-update) | async-done | bytes 2097168 | tf_op jit(solution)/shard_map/all_gather | solution.py:103
  201.8 50.6 %while.34 = (s32[]{:T(128)}, f32[1,8,5,128]{3,2,1,0:T(8,128)S(1)}, f32[1,8,5,128]{3,2,1,0:T(8,128)}, f32[1,128,8,5,128]{1,4,3,2,0:T(8,128)}, s32[2,512]{1,0:T(2,...) while((s32[]{:T(128)}, f32[1,8,5,128]{3,2,1,0:T(8,128)S(1)}, ...), condition=%wide.region_9.10_spmd.clone, body=%wide.region_5.9_spmd.clone.sunk | while | flops 1372491392 | bytes 80563432 | solution.py:128
  201.8 0.7 select_reduce_fusion.4
  202.6 0.2 compare_and_fusion.2
  202.8 1.7 constant_dynamic-slice_fusion.10
  204.5 0.5 copy.64
  205.1 7.2 %fusion.60 = (f32[8,5,128]{2,1,0:T(8,128)S(1)}, f32[8,512,128,5]{2,1,3,0:T(8,128)}) fusion(pred[128,512]{0,1:T(8,128)(4,1)S(1)} %compare_and_fusion.2, bf16[512,8,128,1]{0,2,3,1:T(8,128)(2,1)S(1)} %bitcast.195, bf16[1,128,8,5,128]{4,1,3,2,0:T(8,128)(2,1)} %get-tuple-element.649), kind=kOutput, calls=%fused_computation.36.clone.1 | convolution fusion | flops 678947840 | bytes 12931072 | tf_op jit(solution)/shard_map/while/body/eval_jaxpr/sqgjd,srgd->sgjqr/dot_general | solution.py:115
  212.3 0.6 fusion.61
  212.9 1.4 copy.65
  214.3 9.1 %bitcast_add_fusion.9 = f32[1,128,8,5,128]{1,4,3,2,0:T(8,128)} fusion(f32[1,128,8,5,128]{1,4,3,2,0:T(8,128)} %get-tuple-element.632, bf16[512,8,128,1]{0,2,3,1:T(8,128)(2,1)} %bitcast.196, f32[8,512,128,5]{2,1,3,0:T(8,128)} %get-tuple-element.566, f32[8,5,128]{2,1,0:T(8,128)S(1)} %bitcast.198, pred[128,512]{0,1:T(8,128)(4,1)S(1)} %compare_and_fusion.2, ...), kind=kOutput, calls=%fused_computation.47.clone.1 | convolution fusion | flops 682885120 | bytes 16883712 | tf_op jit(solution)/shard_map/while/body/eval_jaxpr/sgjqr,srgd->sqgjd/dot_general | solution.py:27
  223.4 0.0 slice-done
  223.4 0.0 slice-done.2
  223.5 2.3 fusion.62
  225.7 1.4 bitcast_add_fusion.8
  227.1 0.7 select_reduce_fusion.4
  227.9 0.2 compare_and_fusion.2
  228.1 1.7 constant_dynamic-slice_fusion.10
  229.9 0.5 copy.64
  230.4 7.2 %fusion.60 = (f32[8,5,128]{2,1,0:T(8,128)S(1)}, f32[8,512,128,5]{2,1,3,0:T(8,128)}) fusion(pred[128,512]{0,1:T(8,128)(4,1)S(1)} %compare_and_fusion.2, bf16[512,8,128,1]{0,2,3,1:T(8,128)(2,1)S(1)} %bitcast.195, bf16[1,128,8,5,128]{4,1,3,2,0:T(8,128)(2,1)} %get-tuple-element.649), kind=kOutput, calls=%fused_computation.36.clone.1 | convolution fusion | flops 678947840 | bytes 12931072 | tf_op jit(solution)/shard_map/while/body/eval_jaxpr/sqgjd,srgd->sgjqr/dot_general | solution.py:115
  237.6 0.6 fusion.61
  238.3 1.4 copy.65
  239.6 9.1 %bitcast_add_fusion.9 = f32[1,128,8,5,128]{1,4,3,2,0:T(8,128)} fusion(f32[1,128,8,5,128]{1,4,3,2,0:T(8,128)} %get-tuple-element.632, bf16[512,8,128,1]{0,2,3,1:T(8,128)(2,1)} %bitcast.196, f32[8,512,128,5]{2,1,3,0:T(8,128)} %get-tuple-element.566, f32[8,5,128]{2,1,0:T(8,128)S(1)} %bitcast.198, pred[128,512]{0,1:T(8,128)(4,1)S(1)} %compare_and_fusion.2, ...), kind=kOutput, calls=%fused_computation.47.clone.1 | convolution fusion | flops 682885120 | bytes 16883712 | tf_op jit(solution)/shard_map/while/body/eval_jaxpr/sgjqr,srgd->sqgjd/dot_general | solution.py:27
  248.8 2.3 fusion.62
  251.0 1.4 bitcast_add_fusion.8
  252.4 2.1 select_convert_fusion
  254.6 1.4 copy.45
  (51 shorter events, 0.3 us)
Async XLA Ops:
  6.5 1.0 copy-start
  6.5 71.8 %copy-start.1 = (bf16[1,128,5120]{2,1,0:T(8,128)(2,1)S(1)}, bf16[1,128,5120]{2,1,0:T(8,128)(2,1)}, u32[]{:S(2)}) copy-start(bf16[1,128,5120]{2,1,0:T(8,128)(2,1)} %param.12) | copy-start | bytes 3932164
  6.5 74.7 %all-gather.5.cloned.1.call-start = ((), (), s32[]{:S(2)}) async-start(), calls=%async_computation | async-start | bytes 2621440 | tf_op jit(solution)/shard_map/all_gather | solution.py:65
  42.8 58.1 %all-gather.7.cloned.1.call-start = ((), (), s32[]{:S(2)}) async-start(), calls=%async_computation.1 | async-start | bytes 2621440 | tf_op jit(solution)/shard_map/all_gather | solution.py:66
  76.9 75.3 %all-gather.9.cloned.1.call-start = ((), (), s32[]{:S(2)}) async-start(), calls=%async_computation.2 | async-start | bytes 2359296 | tf_op jit(solution)/shard_map/all_gather | solution.py:102
  77.6 124.2 %all-gather.11.cloned.1.call-start = ((), (), s32[]{:S(2)}) async-start(), calls=%async_computation.3 | async-start | bytes 2359296 | tf_op jit(solution)/shard_map/all_gather | solution.py:103
  78.3 22.6 %copy-start.2 = (s32[1,1,8]{2,1,0:T(1,128)S(1)}, s32[1,1,8]{2,1,0:T(1,128)}, u32[]{:S(2)}) copy-start(s32[1,1,8]{2,1,0:T(1,128)} %param.17) | copy-start | bytes 100
  110.0 9.8 %slice-start.3 = ((s8[10485760]{0:T(1024)(128)(4,1)}), s8[2097152]{0:T(1024)(128)(4,1)S(1)}, s32[]{:S(2)}) async-start(s8[10485760]{0:T(1024)(128)(4,1)} %bitcast.192), calls=%async_computation.7 | async-start | bytes 4194304 | tf_op jit(solution)/shard_map/while
  111.4 8.5 %slice-start.4 = ((s8[10485760]{0:T(1024)(128)(4,1)}), s8[4194304]{0:T(1024)(128)(4,1)S(1)}, s32[]{:S(2)}) async-start(s8[10485760]{0:T(1024)(128)(4,1)} %bitcast.192), calls=%async_computation.8 | async-start | bytes 8388608 | tf_op jit(solution)/shard_map/while
  111.4 8.5 %slice-start.5 = ((s8[10485760]{0:T(1024)(128)(4,1)}), s8[4194304]{0:T(1024)(128)(4,1)S(1)}, s32[]{:S(2)}) async-start(s8[10485760]{0:T(1024)(128)(4,1)} %bitcast.192), calls=%async_computation.9 | async-start | bytes 8388608 | tf_op jit(solution)/shard_map/while
  132.0 10.6 %slice-start.3 = ((s8[10485760]{0:T(1024)(128)(4,1)}), s8[2097152]{0:T(1024)(128)(4,1)S(1)}, s32[]{:S(2)}) async-start(s8[10485760]{0:T(1024)(128)(4,1)} %bitcast.192), calls=%async_computation.7 | async-start | bytes 4194304 | tf_op jit(solution)/shard_map/while
  133.3 9.2 %slice-start.4 = ((s8[10485760]{0:T(1024)(128)(4,1)}), s8[4194304]{0:T(1024)(128)(4,1)S(1)}, s32[]{:S(2)}) async-start(s8[10485760]{0:T(1024)(128)(4,1)} %bitcast.192), calls=%async_computation.8 | async-start | bytes 8388608 | tf_op jit(solution)/shard_map/while
  133.3 9.2 %slice-start.5 = ((s8[10485760]{0:T(1024)(128)(4,1)}), s8[4194304]{0:T(1024)(128)(4,1)S(1)}, s32[]{:S(2)}) async-start(s8[10485760]{0:T(1024)(128)(4,1)} %bitcast.192), calls=%async_computation.9 | async-start | bytes 8388608 | tf_op jit(solution)/shard_map/while
  212.9 10.5 %slice-start = ((s8[10485760]{0:T(1024)(128)(4,1)}), s8[2097152]{0:T(1024)(128)(4,1)S(1)}, s32[]{:S(2)}) async-start(s8[10485760]{0:T(1024)(128)(4,1)} %bitcast.190), calls=%async_computation.4 | async-start | bytes 4194304 | tf_op jit(solution)/shard_map/while
  214.3 9.1 %slice-start.1 = ((s8[10485760]{0:T(1024)(128)(4,1)}), s8[4194304]{0:T(1024)(128)(4,1)S(1)}, s32[]{:S(2)}) async-start(s8[10485760]{0:T(1024)(128)(4,1)} %bitcast.190), calls=%async_computation.5 | async-start | bytes 8388608 | tf_op jit(solution)/shard_map/while
  214.3 9.1 %slice-start.2 = ((s8[10485760]{0:T(1024)(128)(4,1)}), s8[4194304]{0:T(1024)(128)(4,1)S(1)}, s32[]{:S(2)}) async-start(s8[10485760]{0:T(1024)(128)(4,1)} %bitcast.190), calls=%async_computation.6 | async-start | bytes 8388608 | tf_op jit(solution)/shard_map/while
  238.3 10.5 %slice-start = ((s8[10485760]{0:T(1024)(128)(4,1)}), s8[2097152]{0:T(1024)(128)(4,1)S(1)}, s32[]{:S(2)}) async-start(s8[10485760]{0:T(1024)(128)(4,1)} %bitcast.190), calls=%async_computation.4 | async-start | bytes 4194304 | tf_op jit(solution)/shard_map/while
  239.6 9.1 %slice-start.1 = ((s8[10485760]{0:T(1024)(128)(4,1)}), s8[4194304]{0:T(1024)(128)(4,1)S(1)}, s32[]{:S(2)}) async-start(s8[10485760]{0:T(1024)(128)(4,1)} %bitcast.190), calls=%async_computation.5 | async-start | bytes 8388608 | tf_op jit(solution)/shard_map/while
  239.6 9.1 %slice-start.2 = ((s8[10485760]{0:T(1024)(128)(4,1)}), s8[4194304]{0:T(1024)(128)(4,1)S(1)}, s32[]{:S(2)}) async-start(s8[10485760]{0:T(1024)(128)(4,1)} %bitcast.190), calls=%async_computation.6 | async-start | bytes 8388608 | tf_op jit(solution)/shard_map/while
Sparse Core Ops, SparseCore 0:
  42.9 23.6 all-gather.4
  77.0 23.8 all-gather.6
  103.0 49.0 all-gather.8
  154.2 47.5 all-gather.10
where the time goes:
time: 263 us
  waiting for transfers between devices  76.5 us (29%)
  blocking collectives  68.5 us (26%)
  matrix products  63.9 us (24%)
  local copies, waits for them, and re-layouts  20 us (8%)
  other arithmetic  19.6 us (7%)
  between operations  13.9 us (5%)
    all_gather x1, waiting for transfers between devices, shards(): value_rows = lax.all_gather(suffix_values, 'seq', axis=1, tiled=True)  49.6 us
    dot_general x4, matrix products, softmax_step(): jnp.einsum(form, rounded, value_rows, preferred_element_type=jnp.float32)  35.9 us
    all_gather x1, blocking collectives, shards(): lax.all_gather(own_keys, 'seq', axis=0, tiled=True)  35.3 us
    all_gather x1, blocking collectives, shards(): lax.all_gather(own_values, 'seq', axis=0, tiled=True)  33.2 us
    all_gather x1, waiting for transfers between devices, shards(): lax.all_gather(shares[1], 'samp', axis=0, tiled=True)  19.7 us
    dot_general x2, matrix products, suffix_one_step(): jnp.einsum('sqgjd,srgd->sgjqr', query_grid, key_grid, preferred_element_t...  14.5 us
    dot_general x2, matrix products, prefix_one_step(): jnp.einsum('sqgjd,rgd->sgjqr', query_grid, key_grid, preferred_element_ty...  13.5 us
    reduce_sum x4, other arithmetic, softmax_step(): new_sum = run_sum * scale_old + jnp.sum(weights, axis=-1)  9.15 us
  transfers between devices with their start and end apart: 4, of which 3 were waited for; matrix products, arithmetic and copies ran while one was open for 18% of the time, Pallas kernels for 0%

commit v1 on v0

--- a/solution.py
+++ b/solution.py
@@ -99,8 +99,11 @@
         ),
     )
     suffix_carry = carry
-    key_rows = lax.all_gather(suffix_keys, "seq", axis=1, tiled=True)
-    value_rows = lax.all_gather(suffix_values, "seq", axis=1, tiled=True)
+    key_rows, value_rows = jnp.split(
+        lax.all_gather(jnp.concatenate([suffix_keys, suffix_values], 0), "seq", tiled=True, axis=1),
+        [suffix_keys.shape[0]],
+        0,
+    )
     count = key_rows.shape[1]
     size = block_size(count)
     steps = count // size

time: 263 us -> 240 us (0.913)
  waiting for transfers between devices: 76.5 us -> 49.4 us
  local copies, waits for them, and re-layouts: 20 us -> 24.5 us
    all_gather x2 -> x1, waiting for transfers between devices: 55.5 us -> 29.3 us  [shards(): lax.all_gather(jnp.concatenate([suffix_keys, suffix_values], 0), 'seq', t...]
    split x0 -> x1, local copies, waits for them, and re-layouts: none -> 4.63 us  [shards(): jnp.split(lax.all_gather(jnp.concatenate([suffix_keys, suffix_values], 0)...]
  transfers between devices with their start and end apart: 4 -> 3, of which waited for: 3 -> 2; matrix products, arithmetic and copies ran while one was open for 18% -> 21% of each run, Pallas kernels for 0% -> 0%
where the time goes in v1:
time: 240 us
  blocking collectives  68.5 us (29%)
  matrix products  64 us (27%)
  waiting for transfers between devices  49.4 us (21%)
  local copies, waits for them, and re-layouts  24.5 us (10%)
  other arithmetic  19.2 us (8%)
  between operations  13.9 us (6%)
    dot_general x4, matrix products, softmax_step(): jnp.einsum(form, rounded, value_rows, preferred_element_type=jnp.float32)  36.2 us
    all_gather x1, blocking collectives, shards(): lax.all_gather(own_keys, 'seq', axis=0, tiled=True)  35.3 us
    all_gather x1, blocking collectives, shards(): lax.all_gather(own_values, 'seq', axis=0, tiled=True)  33.2 us
    all_gather x1, waiting for transfers between devices, shards(): lax.all_gather(jnp.concatenate([suffix_keys, suffix_values], 0), 'seq', t...  29.3 us
    all_gather x1, waiting for transfers between devices, shards(): lax.all_gather(shares[1], 'samp', axis=0, tiled=True)  20 us
    dot_general x2, matrix products, suffix_one_step(): jnp.einsum('sqgjd,srgd->sgjqr', query_grid, key_grid, preferred_element_t...  14.5 us
    dot_general x2, matrix products, prefix_one_step(): jnp.einsum('sqgjd,rgd->sgjqr', query_grid, key_grid, preferred_element_ty...  13.3 us
    reduce_sum x4, other arithmetic, softmax_step(): new_sum = run_sum * scale_old + jnp.sum(weights, axis=-1)  9.15 us
  transfers between devices with their start and end apart: 3, of which 2 were waited for; matrix products, arithmetic and copies ran while one was open for 21% of the time, Pallas kernels for 0%

profile of v1, /device:TPU:0, one launch (start us, length us, event | category | flops | bytes accessed | tf_op | source)
XLA Modules:
  0.0 239.7 jit_solution(15917443136913775346)
XLA Ops:
  6.5 0.0 all-gather.4.cloned.1.call-start
  6.6 0.9 copy-done
  7.5 35.3 %all_gather.15 = bf16[256,1024]{1,0:T(8,128)(2,1)} all-gather(bf16[32,1024]{1,0:T(8,128)(2,1)S(1)} %constant_dynamic-slice_fusion.6), channel_id=1, replica_groups=mesh['seq'=8,'samp'=4] {'seq'}, dimensions={0}, use_global_device_ids=true | all-gather | bytes 589824 | tf_op jit(solution)/shard_map/all_gather | solution.py:61
  42.7 0.0 all-gather.4.cloned.1.call-update
  42.8 0.0 all-gather.6.cloned.1.call-start
  42.8 0.9 constant_dynamic-slice_fusion.5
  43.7 33.2 %all_gather.17 = bf16[256,1024]{1,0:T(8,128)(2,1)} all-gather(bf16[32,1024]{1,0:T(8,128)(2,1)S(1)} %constant_dynamic-slice_fusion.5), channel_id=1, replica_groups=mesh['seq'=8,'samp'=4] {'seq'}, dimensions={0}, use_global_device_ids=true | all-gather | bytes 589824 | tf_op jit(solution)/shard_map/all_gather | solution.py:62
  76.9 0.0 all-gather.6.cloned.1.call-update
  76.9 0.0 all-gather.8.cloned.1.call-start
  77.0 0.9 pad_maximum_fusion
  77.8 0.0 all-gather.8.cloned.1.call-update
  77.9 0.0 copy-start.4
  77.9 0.8 copy.39
  78.7 1.4 copy.41
  80.9 0.0 all-gather.4.cloned.1.call-done
  80.9 20.0 %all-gather.6.cloned.1.call-done = bf16[1024,1024]{1,0:T(8,128)(2,1)} async-done(((bf16[256,1024]{1,0:T(8,128)(2,1)}), bf16[1024,1024]{1,0:T(8,128)(2,1)}) %all-gather.6.cloned.1.call-update) | async-done | bytes 2097168 | tf_op jit(solution)/shard_map/all_gather | solution.py:66
  100.9 45.7 %while.35 = (s32[]{:T(128)}, f32[1,8,5,128]{3,2,1,0:T(8,128)S(1)}, f32[1,8,5,128]{3,2,1,0:T(8,128)}, f32[1,128,8,5,128]{1,4,3,2,0:T(8,128)}, s32[2,512]{1,0:T(2,...) while((s32[]{:T(128)}, f32[1,8,5,128]{3,2,1,0:T(8,128)S(1)}, ...), condition=%wide.region_4.5_spmd.clone, body=%wide.region_0.4_spmd.clone.sunk | while | flops 1373029888 | bytes 80294112 | solution.py:92
  100.9 0.1 select_reduce_fusion.5
  101.0 1.7 constant_dynamic-slice_fusion.11
  102.7 0.5 copy.67
  103.3 6.7 %fusion.67 = (f32[8,5,128]{2,1,0:T(8,128)S(1)}, f32[8,512,128,5]{2,1,3,0:T(8,128)}) fusion(pred[512]{0:T(512)(128)(4,1)S(1)} %broadcast_compare_fusion.5, bf16[512,8,128,1]{0,2,3,1:T(8,128)(2,1)S(1)} %bitcast.194, bf16[1,128,8,5,128]{4,1,3,2,0:T(8,128)(2,1)} %get-tuple-element.615), kind=kOutput, calls=%fused_computation.3.clone.1 | convolution fusion | flops 678947840 | bytes 12866048 | tf_op jit(solution)/shard_map/while/body/eval_jaxpr/sqgjd,rgd->sgjqr/dot_general | solution.py:84
  110.0 0.0 slice-start.3
  110.0 1.4 copy.68
  111.4 8.5 %bitcast_add_fusion.11 = f32[1,128,8,5,128]{1,4,3,2,0:T(8,128)} fusion(f32[1,128,8,5,128]{1,4,3,2,0:T(8,128)} %get-tuple-element.600, bf16[512,8,128,1]{0,2,3,1:T(8,128)(2,1)} %bitcast.197, f32[8,512,128,5]{2,1,3,0:T(8,128)} %get-tuple-element.583, f32[8,5,128]{2,1,0:T(8,128)S(1)} %bitcast.202, pred[512]{0:T(512)(128)(4,1)S(1)} %broadcast_compare_fusion.5, ...), kind=kOutput, calls=%fused_computation.14.clone.1 | convolution fusion | flops 683540480 | bytes 16818688 | tf_op jit(solution)/shard_map/while/body/eval_jaxpr/sgjqr,rgd->sqgjd/dot_general | solution.py:27
  119.9 0.0 slice-done.4
  119.9 2.3 fusion.69
  122.2 0.6 bitcast_add_fusion.10
  122.8 0.1 select_reduce_fusion.5
  122.9 1.7 constant_dynamic-slice_fusion.11
  124.7 0.5 copy.67
  125.2 6.6 %fusion.67 = (f32[8,5,128]{2,1,0:T(8,128)S(1)}, f32[8,512,128,5]{2,1,3,0:T(8,128)}) fusion(pred[512]{0:T(512)(128)(4,1)S(1)} %broadcast_compare_fusion.5, bf16[512,8,128,1]{0,2,3,1:T(8,128)(2,1)S(1)} %bitcast.194, bf16[1,128,8,5,128]{4,1,3,2,0:T(8,128)(2,1)} %get-tuple-element.615), kind=kOutput, calls=%fused_computation.3.clone.1 | convolution fusion | flops 678947840 | bytes 12866048 | tf_op jit(solution)/shard_map/while/body/eval_jaxpr/sqgjd,rgd->sgjqr/dot_general | solution.py:84
  131.9 0.0 slice-start.3
  131.9 1.4 copy.68
  133.3 9.6 %bitcast_add_fusion.11 = f32[1,128,8,5,128]{1,4,3,2,0:T(8,128)} fusion(f32[1,128,8,5,128]{1,4,3,2,0:T(8,128)} %get-tuple-element.600, bf16[512,8,128,1]{0,2,3,1:T(8,128)(2,1)} %bitcast.197, f32[8,512,128,5]{2,1,3,0:T(8,128)} %get-tuple-element.583, f32[8,5,128]{2,1,0:T(8,128)S(1)} %bitcast.202, pred[512]{0:T(512)(128)(4,1)S(1)} %broadcast_compare_fusion.5, ...), kind=kOutput, calls=%fused_computation.14.clone.1 | convolution fusion | flops 683540480 | bytes 16818688 | tf_op jit(solution)/shard_map/while/body/eval_jaxpr/sgjqr,rgd->sqgjd/dot_general | solution.py:27
  142.9 0.0 slice-done.5
  142.9 2.3 fusion.69
  145.2 1.4 bitcast_add_fusion.10
  146.6 29.3 %all-gather.8.cloned.1.call-done = bf16[2,1024,1024]{2,1,0:T(8,128)(2,1)} async-done(((bf16[2,128,1024]{2,1,0:T(8,128)(2,1)}), bf16[2,1024,1024]{2,1,0:T(8,128)(2,1)}) %all-gather.8.cloned.1.call-update) | async-done | bytes 4194320 | tf_op jit(solution)/shard_map/all_gather | solution.py:103
  175.9 4.6 %fusion.41 = (bf16[1,1024,1024]{2,1,0:T(8,128)(2,1)}, bf16[1,1024,1024]{2,1,0:T(8,128)(2,1)}) fusion(bf16[2,1024,1024]{2,1,0:T(8,128)(2,1)} %all-gather.8.cloned.1.call-done), kind=kLoop, calls=%fused_computation.85 | loop fusion | bytes 8388608 | tf_op jit(solution)/shard_map/split | solution.py:102
  180.6 49.1 %while.34 = (s32[]{:T(128)}, f32[1,8,5,128]{3,2,1,0:T(8,128)S(1)}, f32[1,8,5,128]{3,2,1,0:T(8,128)}, f32[1,128,8,5,128]{1,4,3,2,0:T(8,128)}, s32[2,512]{1,0:T(2,...) while((s32[]{:T(128)}, f32[1,8,5,128]{3,2,1,0:T(8,128)S(1)}, ...), condition=%wide.region_9.10_spmd.clone, body=%wide.region_5.9_spmd.clone.sunk | while | flops 1372491392 | bytes 80563432 | solution.py:131
  180.6 0.1 select_reduce_fusion.4
  180.7 0.2 compare_and_fusion.2
  180.9 1.7 constant_dynamic-slice_fusion.10
  182.6 0.5 copy.65
  183.2 7.2 %fusion.61 = (f32[8,5,128]{2,1,0:T(8,128)S(1)}, f32[8,512,128,5]{2,1,3,0:T(8,128)}) fusion(pred[128,512]{0,1:T(8,128)(4,1)S(1)} %compare_and_fusion.2, bf16[512,8,128,1]{0,2,3,1:T(8,128)(2,1)S(1)} %bitcast.195, bf16[1,128,8,5,128]{4,1,3,2,0:T(8,128)(2,1)} %get-tuple-element.651), kind=kOutput, calls=%fused_computation.36.clone.1 | convolution fusion | flops 678947840 | bytes 12931072 | tf_op jit(solution)/shard_map/while/body/eval_jaxpr/sqgjd,srgd->sgjqr/dot_general | solution.py:118
  190.4 0.6 fusion.62
  191.0 1.3 copy.66
  192.4 9.0 %bitcast_add_fusion.9 = f32[1,128,8,5,128]{1,4,3,2,0:T(8,128)} fusion(f32[1,128,8,5,128]{1,4,3,2,0:T(8,128)} %get-tuple-element.634, bf16[512,8,128,1]{0,2,3,1:T(8,128)(2,1)} %bitcast.196, f32[8,512,128,5]{2,1,3,0:T(8,128)} %get-tuple-element.568, f32[8,5,128]{2,1,0:T(8,128)S(1)} %bitcast.200, pred[128,512]{0,1:T(8,128)(4,1)S(1)} %compare_and_fusion.2, ...), kind=kOutput, calls=%fused_computation.47.clone.1 | convolution fusion | flops 682885120 | bytes 16883712 | tf_op jit(solution)/shard_map/while/body/eval_jaxpr/sgjqr,srgd->sqgjd/dot_general | solution.py:27
  201.4 0.0 slice-done.1
  201.4 2.3 fusion.63
  203.7 1.4 bitcast_add_fusion.8
  205.1 0.1 select_reduce_fusion.4
  205.2 0.2 compare_and_fusion.2
  205.4 1.7 constant_dynamic-slice_fusion.10
  207.2 0.5 copy.65
  207.7 7.2 %fusion.61 = (f32[8,5,128]{2,1,0:T(8,128)S(1)}, f32[8,512,128,5]{2,1,3,0:T(8,128)}) fusion(pred[128,512]{0,1:T(8,128)(4,1)S(1)} %compare_and_fusion.2, bf16[512,8,128,1]{0,2,3,1:T(8,128)(2,1)S(1)} %bitcast.195, bf16[1,128,8,5,128]{4,1,3,2,0:T(8,128)(2,1)} %get-tuple-element.651), kind=kOutput, calls=%fused_computation.36.clone.1 | convolution fusion | flops 678947840 | bytes 12931072 | tf_op jit(solution)/shard_map/while/body/eval_jaxpr/sqgjd,srgd->sgjqr/dot_general | solution.py:118
  214.9 0.6 fusion.62
  215.6 1.3 copy.66
  216.9 9.0 %bitcast_add_fusion.9 = f32[1,128,8,5,128]{1,4,3,2,0:T(8,128)} fusion(f32[1,128,8,5,128]{1,4,3,2,0:T(8,128)} %get-tuple-element.634, bf16[512,8,128,1]{0,2,3,1:T(8,128)(2,1)} %bitcast.196, f32[8,512,128,5]{2,1,3,0:T(8,128)} %get-tuple-element.568, f32[8,5,128]{2,1,0:T(8,128)S(1)} %bitcast.200, pred[128,512]{0,1:T(8,128)(4,1)S(1)} %compare_and_fusion.2, ...), kind=kOutput, calls=%fused_computation.47.clone.1 | convolution fusion | flops 682885120 | bytes 16883712 | tf_op jit(solution)/shard_map/while/body/eval_jaxpr/sgjqr,srgd->sqgjd/dot_general | solution.py:27
  225.9 0.0 slice-done.2
  225.9 2.3 fusion.63
  228.2 1.4 bitcast_add_fusion.8
  229.6 2.1 select_convert_fusion
  231.7 1.4 copy.46
  (56 shorter events, 0.3 us)
Async XLA Ops:
  6.5 1.0 copy-start
  6.5 70.4 %copy-start.3 = (bf16[1,128,1024]{2,1,0:T(8,128)(2,1)S(1)}, bf16[1,128,1024]{2,1,0:T(8,128)(2,1)}, u32[]{:S(2)}) copy-start(bf16[1,128,1024]{2,1,0:T(8,128)(2,1)} %param.15) | copy-start | bytes 786436
  6.5 70.4 %copy-start.2 = (bf16[1,128,1024]{2,1,0:T(8,128)(2,1)S(1)}, bf16[1,128,1024]{2,1,0:T(8,128)(2,1)}, u32[]{:S(2)}) copy-start(bf16[1,128,1024]{2,1,0:T(8,128)(2,1)} %param.16) | copy-start | bytes 786436
  6.5 71.3 %copy-start.1 = (bf16[1,128,5120]{2,1,0:T(8,128)(2,1)S(1)}, bf16[1,128,5120]{2,1,0:T(8,128)(2,1)}, u32[]{:S(2)}) copy-start(bf16[1,128,5120]{2,1,0:T(8,128)(2,1)} %param.12) | copy-start | bytes 3932164
  6.5 74.3 %all-gather.4.cloned.1.call-start = ((), (), s32[]{:S(2)}) async-start(), calls=%async_computation | async-start | bytes 2621440 | tf_op jit(solution)/shard_map/all_gather | solution.py:65
  42.8 58.1 %all-gather.6.cloned.1.call-start = ((), (), s32[]{:S(2)}) async-start(), calls=%async_computation.1 | async-start | bytes 2621440 | tf_op jit(solution)/shard_map/all_gather | solution.py:66
  76.9 99.0 %all-gather.8.cloned.1.call-start = ((), (), s32[]{:S(2)}) async-start(), calls=%async_computation.2 | async-start | bytes 4718592 | tf_op jit(solution)/shard_map/all_gather | solution.py:103
  77.9 23.0 %copy-start.4 = (s32[1,1,8]{2,1,0:T(1,128)S(1)}, s32[1,1,8]{2,1,0:T(1,128)}, u32[]{:S(2)}) copy-start(s32[1,1,8]{2,1,0:T(1,128)} %param.17) | copy-start | bytes 100
  110.0 9.9 %slice-start.3 = ((s8[10485760]{0:T(1024)(128)(4,1)}), s8[2097152]{0:T(1024)(128)(4,1)S(1)}, s32[]{:S(2)}) async-start(s8[10485760]{0:T(1024)(128)(4,1)} %bitcast.192), calls=%async_computation.6 | async-start | bytes 4194304 | tf_op jit(solution)/shard_map/while
  111.4 8.5 %slice-start.4 = ((s8[10485760]{0:T(1024)(128)(4,1)}), s8[4194304]{0:T(1024)(128)(4,1)S(1)}, s32[]{:S(2)}) async-start(s8[10485760]{0:T(1024)(128)(4,1)} %bitcast.192), calls=%async_computation.7 | async-start | bytes 8388608 | tf_op jit(solution)/shard_map/while
  111.4 8.5 %slice-start.5 = ((s8[10485760]{0:T(1024)(128)(4,1)}), s8[4194304]{0:T(1024)(128)(4,1)S(1)}, s32[]{:S(2)}) async-start(s8[10485760]{0:T(1024)(128)(4,1)} %bitcast.192), calls=%async_computation.8 | async-start | bytes 8388608 | tf_op jit(solution)/shard_map/while
  131.9 11.0 %slice-start.3 = ((s8[10485760]{0:T(1024)(128)(4,1)}), s8[2097152]{0:T(1024)(128)(4,1)S(1)}, s32[]{:S(2)}) async-start(s8[10485760]{0:T(1024)(128)(4,1)} %bitcast.192), calls=%async_computation.6 | async-start | bytes 4194304 | tf_op jit(solution)/shard_map/while
  133.3 9.6 %slice-start.4 = ((s8[10485760]{0:T(1024)(128)(4,1)}), s8[4194304]{0:T(1024)(128)(4,1)S(1)}, s32[]{:S(2)}) async-start(s8[10485760]{0:T(1024)(128)(4,1)} %bitcast.192), calls=%async_computation.7 | async-start | bytes 8388608 | tf_op jit(solution)/shard_map/while
  133.3 9.6 %slice-start.5 = ((s8[10485760]{0:T(1024)(128)(4,1)}), s8[4194304]{0:T(1024)(128)(4,1)S(1)}, s32[]{:S(2)}) async-start(s8[10485760]{0:T(1024)(128)(4,1)} %bitcast.192), calls=%async_computation.8 | async-start | bytes 8388608 | tf_op jit(solution)/shard_map/while
  146.6 34.0 %copy-start.5 = (s32[1,1,8]{2,1,0:T(1,128)S(1)}, s32[1,1,8]{2,1,0:T(1,128)}, u32[]{:S(2)}) copy-start(s32[1,1,8]{2,1,0:T(1,128)} %param.18) | copy-start | bytes 100
  191.0 10.3 %slice-start = ((s8[10485760]{0:T(1024)(128)(4,1)}), s8[2097152]{0:T(1024)(128)(4,1)S(1)}, s32[]{:S(2)}) async-start(s8[10485760]{0:T(1024)(128)(4,1)} %bitcast.190), calls=%async_computation.3 | async-start | bytes 4194304 | tf_op jit(solution)/shard_map/while
  192.4 9.0 %slice-start.1 = ((s8[10485760]{0:T(1024)(128)(4,1)}), s8[4194304]{0:T(1024)(128)(4,1)S(1)}, s32[]{:S(2)}) async-start(s8[10485760]{0:T(1024)(128)(4,1)} %bitcast.190), calls=%async_computation.4 | async-start | bytes 8388608 | tf_op jit(solution)/shard_map/while
  192.4 9.0 %slice-start.2 = ((s8[10485760]{0:T(1024)(128)(4,1)}), s8[4194304]{0:T(1024)(128)(4,1)S(1)}, s32[]{:S(2)}) async-start(s8[10485760]{0:T(1024)(128)(4,1)} %bitcast.190), calls=%async_computation.5 | async-start | bytes 8388608 | tf_op jit(solution)/shard_map/while
  215.6 10.4 %slice-start = ((s8[10485760]{0:T(1024)(128)(4,1)}), s8[2097152]{0:T(1024)(128)(4,1)S(1)}, s32[]{:S(2)}) async-start(s8[10485760]{0:T(1024)(128)(4,1)} %bitcast.190), calls=%async_computation.3 | async-start | bytes 4194304 | tf_op jit(solution)/shard_map/while
  216.9 9.0 %slice-start.1 = ((s8[10485760]{0:T(1024)(128)(4,1)}), s8[4194304]{0:T(1024)(128)(4,1)S(1)}, s32[]{:S(2)}) async-start(s8[10485760]{0:T(1024)(128)(4,1)} %bitcast.190), calls=%async_computation.4 | async-start | bytes 8388608 | tf_op jit(solution)/shard_map/while
  216.9 9.0 %slice-start.2 = ((s8[10485760]{0:T(1024)(128)(4,1)}), s8[4194304]{0:T(1024)(128)(4,1)S(1)}, s32[]{:S(2)}) async-start(s8[10485760]{0:T(1024)(128)(4,1)} %bitcast.190), calls=%async_computation.5 | async-start | bytes 8388608 | tf_op jit(solution)/shard_map/while
Sparse Core Ops, SparseCore 0:
  42.9 23.6 all-gather.3
  77.0 23.8 all-gather.5
  103.1 72.7 all-gather.7
